TPU v7x, 16 devices: a 4x2x1 block of a 4x4x8 slice. The times are simulated.
16 devices in a mesh: dp: 2 (over y, z), tp: 8 (over x, core).
Axes of the slice: x: 4, y: 2, z: 1, core: 2. Of those that a mesh axis runs over, the one named last changes fastest.
The devices are a block of a 4x4x8 slice.
Arguments:
- x: bfloat16 [4096, 4096], P(('dp', 'tp')), parts along dimension 0
- w_gate: bfloat16 [4096, 12288], P(None, 'tp')
- w_up: bfloat16 [4096, 12288], P(None, 'tp')
- w_down: bfloat16 [12288, 4096], P('tp')
Outputs:
- output: bfloat16 [4096, 4096], P(('dp', 'tp')), parts along dimension 0
There are 2 independent parts. A program takes and returns all parts, laid end to end along the dimension named above; an argument that names none is the same for every part.
All inputs are finite; a program needn't handle non-finite values.
Results may differ from a plain program's by a relative error of at most 0.016.
Values are sent between devices in bfloat16 or wider.
A program may use at most 768 MiB of HBM per device.

v0:
```python
import jax
import jax.numpy as jnp
from jax import lax
from jax.sharding import PartitionSpec as P


def solution(mesh):
    def step(x, w_gate, w_up, w_down):
        rows = lax.all_gather(x, "tp", axis=0, tiled=True)
        gate = jnp.dot(rows, w_gate, preferred_element_type=jnp.float32)
        up = jnp.dot(rows, w_up, preferred_element_type=jnp.float32)
        hidden = (jax.nn.silu(gate) * up).astype(jnp.bfloat16)
        term = jnp.dot(hidden, w_down, preferred_element_type=jnp.float32).astype(jnp.bfloat16)
        return lax.psum_scatter(term, "tp", scatter_dimension=0, tiled=True)

    return jax.shard_map(
        step,
        mesh=mesh,
        in_specs=(P(("dp", "tp"), None), P(None, "tp"), P(None, "tp"), P("tp", None)),
        out_specs=P(("dp", "tp"), None),
        check_vma=False,
    )
```

profile of v0, /device:TPU:112, one launch (start us, length us, event | category | flops | bytes accessed | tf_op | source)
XLA Modules:
  0.0 290.3 jit_solution(13387651908092023220)
XLA Ops:
  6.5 0.0 all-gather.2.cloned.1.call-start
  6.6 0.7 all-gather.2.cloned.1.call-update
  7.3 0.1 reduce-scatter.2.cloned.1.call-start
  7.4 85.5 %all-gather.2.cloned.1.call-done = bf16[2048,4096]{1,0:T(8,128)(2,1)} async-done(((bf16[256,4096]{1,0:T(8,128)(2,1)}), bf16[2048,4096]{1,0:T(8,128)(2,1)}) %all-gather.2.cloned.1.call-update) | async-done | bytes 16777232 | tf_op jit(solution)/shard_map/all_gather | solution.py:9
  92.9 0.0 copy-start
  92.9 34.2 %fusion = f32[2048,1536]{1,0:T(8,128)} fusion(bf16[2048,4096]{1,0:T(8,128)(2,1)} %all-gather.2.cloned.1.call-done, bf16[4096,1536]{1,0:T(8,128)(2,1)} %param.5), kind=kOutput, calls=%fused_computation.2 | convolution fusion | flops 25769803776 | bytes 41943040 | tf_op jit(solution)/shard_map/dot_general | solution.py:10
  127.1 0.0 copy-done
  127.1 35.1 %multiply_convert_fusion = bf16[2048,1536]{1,0:T(8,128)(2,1)} fusion(f32[2048,1536]{1,0:T(8,128)} %fusion, bf16[2048,4096]{1,0:T(8,128)(2,1)S(1)} %copy-done, bf16[4096,1536]{1,0:T(8,128)(2,1)} %param.6), kind=kOutput, calls=%fused_computation.1 | convolution fusion | flops 25788678144 | bytes 48234496 | tf_op jit(solution)/shard_map/dot_general | solution.py:11
  162.3 32.7 %convolution_convert_fusion = bf16[2048,4096]{1,0:T(8,128)(2,1)} fusion(bf16[2048,1536]{1,0:T(8,128)(2,1)} %multiply_convert_fusion, bf16[1536,4096]{1,0:T(8,128)(2,1)} %param.7), kind=kOutput, calls=%fused_computation | convolution fusion | flops 25778192384 | bytes 35651584 | tf_op jit(solution)/shard_map/dot_general | solution.py:13
  195.0 0.1 reduce-scatter.2.cloned.1.call-update
  195.0 88.4 %reduce-scatter.2.cloned.1.call-done = bf16[256,4096]{1,0:T(8,128)(2,1)} async-done(((bf16[2048,4096]{1,0:T(8,128)(2,1)}), bf16[256,4096]{1,0:T(8,128)(2,1)}) %reduce-scatter.2.cloned.1.call-update) | async-done | bytes 2097168 | tf_op jit(solution)/shard_map/reduce_scatter | solution.py:14
Async XLA Ops:
  6.5 86.4 %all-gather.2.cloned.1.call-start = ((), (), s32[]{:S(2)}) async-start(), calls=%async_computation.1 | async-start | bytes 18874368 | tf_op jit(solution)/shard_map/all_gather | solution.py:9
  7.3 276.1 %reduce-scatter.2.cloned.1.call-start = ((), (), s32[]{:S(2)}) async-start(), calls=%async_computation.2 | async-start | bytes 18874368 | tf_op jit(solution)/shard_map/reduce_scatter | solution.py:14
  92.9 34.2 %copy-start = (bf16[2048,4096]{1,0:T(8,128)(2,1)S(1)}, bf16[2048,4096]{1,0:T(8,128)(2,1)}, u32[]{:S(2)}) copy-start(bf16[2048,4096]{1,0:T(8,128)(2,1)} %all-gather.2.cloned.1.call-done) | copy-start | bytes 50331652
Sparse Core Ops, SparseCore 0:
  8.9 83.9 all-gather.1
  195.1 88.2 reduce-scatter.1
where the time goes:
time: 290 us
  waiting for transfers between devices  175 us (60%)
  matrix products  102 us (35%)
  between operations  13.4 us (5%)
    reduce_scatter x1, waiting for transfers between devices, step(): return lax.psum_scatter(term, 'tp', scatter_dimension=0, tiled=True)  88.4 us
    all_gather x1, waiting for transfers between devices, step(): rows = lax.all_gather(x, 'tp', axis=0, tiled=True)  85.5 us
    dot_general x1, matrix products, step(): up = jnp.dot(rows, w_up, preferred_element_type=jnp.float32)  35.1 us
    dot_general x1, matrix products, step(): gate = jnp.dot(rows, w_gate, preferred_element_type=jnp.float32)  34.2 us
    dot_general x1, matrix products, step(): jnp.dot(hidden, w_down, preferred_element_type=jnp.float32)  32.7 us
  transfers between devices with their start and end apart: 2, of which 2 were waited for; matrix products, arithmetic and copies ran while one was open for 0% of the time, Pallas kernels for 0%

commit v1 on v0

v1 whole, which is shorter than its diff:
```python
import functools

import jax
import jax.numpy as jnp
from jax import lax
from jax.experimental import pallas as pl
from jax.experimental.pallas import tpu as pltpu
from jax.sharding import PartitionSpec as P

MESH = pl.DeviceIdType.MESH
AXIS = "tp"
F32 = jnp.float32
BF16 = jnp.bfloat16
VMEM_BYTES = 67043328


def split(total, most):
    return max(t for t in range(256, min(total, most) + 1, 256) if total % t == 0)


def kernel(
    n,
    x, wg, wu, wd,
    y, xg, tp,
    wgv, wuv, wdv, xv, hv, ov, tv, sv, fv, own,
    w_sem, wd_sem, x_sem, t_sem, y_sem,
    ag_send, ag_recv, xd_send, xd_recv, td_send, td_recv,
    dir_send, dir_recv, far_send, far_recv, sum_send, sum_recv,
):
    rows, depth = x.shape
    ff = wg.shape[1]
    h, q = rows // 2, rows // 4
    me = lax.axis_index(AXIS)
    chips = n // 2
    c, k = lax.div(me, 2), lax.rem(me, 2)

    def device(step, core):
        return lax.rem(c + step + chips, chips) * 2 + core

    other = 1 - k
    partner = device(0, other)
    right, left = device(1, k), device(-1, k)
    to = (right, left)
    came = (left, right)

    def at(ref, block, start, size):
        return ref.at[block, pl.ds(start, size), :]

    def remote(src, dst, ssem, rsem, device_id):
        return pltpu.make_async_remote_copy(
            src_ref=src, dst_ref=dst, send_sem=ssem, recv_sem=rsem,
            device_id={AXIS: device_id}, device_id_type=MESH,
        )

    def first(d, j):
        return (0 if d == 0 else h) + j * q

    def second(d, j):
        return (h if d == 0 else 0) + j * q

    def ag(d, t):
        if t in (2, 3):
            r = pl.ds(first(d, t - 2), q)
            src = xg.at[came[d], r, :]
            dst = src
        else:
            r = pl.ds(first(d, t) if t < 2 else second(d, t - 4), q)
            src = x.at[r, :]
            dst = xg.at[me, r, :]
        return remote(src, dst, ag_send.at[d, t], ag_recv.at[d, t], to[d])

    def ag_wait(*ts):
        for t in ts:
            for d in (0, 1):
                ag(d, t).wait_recv()

    def ag_start(*ts):
        for t in ts:
            for d in (0, 1):
                ag(d, t).start()

    far = device(2, k)
    pieces = ((left, 0), (right, h), (far, 0), (far, h), (left, h), (right, 0))

    def xd(i):
        if i == 0:
            src, dst = x, xg.at[me]
        else:
            block, start = pieces[i - 1]
            src = at(xg, block, start, h)
            dst = src
        return remote(src, dst, xd_send.at[i], xd_recv.at[i], partner)

    def td(j, slot):
        return remote(ov.at[slot], tp.at[j], td_send.at[j], td_recv.at[j], partner)

    def direct(d):
        r = pl.ds(h, h) if d == 0 else pl.ds(0, h)
        return remote(ov.at[2, r, :], fv.at[d, r, :], dir_send.at[d], dir_recv.at[d], to[d])

    def distant(d, j):
        return remote(
            at(ov, 1, first(d, j), q), at(sv, d, j * q, q), far_send.at[d, j], far_recv.at[d, j], to[d]
        )

    def summed(d, j):
        return remote(
            at(ov, 2, (2 * j + d) * q, q), at(fv, d, first(d, j), q), sum_send.at[d, j], sum_recv.at[d, j], to[d]
        )

    def load(slot, parts):
        out, place = [], 0
        for i, (src, size) in enumerate(parts):
            out.append(pltpu.make_async_copy(src, xv.at[slot, pl.ds(place, size), :], x_sem.at[slot, i]))
            place += size
        return out

    def near(core):
        return [(at(xg, device(-1, core), 0, h), h), (at(xg, device(1, core), h, h), h)]

    def opposite(core):
        return [(xg.at[device(2, core)], rows)]

    def late(core):
        a, b = device(1, core), device(-1, core)
        return [(at(xg, a, 0, q), q), (at(xg, b, h, q), q), (at(xg, a, q, q), q), (at(xg, b, h + q, q), q)]

    def start(copies):
        for copy in copies:
            copy.start()

    def wait(copies):
        for copy in copies:
            copy.wait()

    def term(j):
        return pltpu.make_async_copy(tp.at[j], tv, t_sem)

    nt = split(ff, 768)
    dt = split(depth, 2048)

    def weights(i):
        r = pl.ds(pl.multiple_of(i * nt, nt), nt)
        return [
            pltpu.make_async_copy(wg.at[:, r], wgv.at[:, r], w_sem.at[0, i]),
            pltpu.make_async_copy(wu.at[:, r], wuv.at[:, r], w_sem.at[1, i]),
        ]

    down = pltpu.make_async_copy(wd, wdv, wd_sem)

    def up(slot, hslot, hook=None, arriving=False):
        def body(i, carry):
            if arriving:
                wait(weights(i))
            if hook is not None:
                pl.when(i == ff // nt - 1)(hook)
            for s in range(0, nt, 256):
                r = pl.ds(pl.multiple_of(i * nt + s, 256), 256)
                a = xv[slot]
                g = jnp.dot(a, wgv[:, r], preferred_element_type=F32)
                u = jnp.dot(a, wuv[:, r], preferred_element_type=F32)
                hv[hslot, :, r] = (g * jax.nn.sigmoid(g) * u).astype(BF16)
            return carry

        lax.fori_loop(0, ff // nt, body, 0)

    def project(hslot, place, size, finish, hook=None):
        def body(i, carry):
            if hook is not None:
                pl.when(i == depth // dt - 1)(hook)
            for s in range(0, dt, 512):
                r = pl.ds(pl.multiple_of(i * dt + s, 512), 512)
                finish(r, jnp.dot(hv[hslot, pl.ds(place, size), :], wdv[:, r], preferred_element_type=F32))
            return carry

        lax.fori_loop(0, depth // dt, body, 0)

    def to_other(slot):
        def finish(r, acc):
            ov[slot, :, r] = acc.astype(BF16)
        return finish

    def to_own(r, acc):
        own[:, r] = acc + tv[:, r].astype(F32)

    def to_ring(slot):
        def finish(r, acc):
            ov[slot, :, r] = (acc + tv[:, r].astype(F32)).astype(BF16)
        return finish

    def to_last(j):
        def finish(r, acc):
            for d in (0, 1):
                place = pl.ds((2 * j + d) * q, q)
                total = acc[d * q:(d + 1) * q] + tv[place, r].astype(F32) + sv[d, pl.ds(j * q, q), r].astype(F32)
                ov[2, place, r] = total.astype(BF16)
        return finish

    load_own = load(0, [(x, rows)])
    start(load_own)
    for i in range(ff // nt):
        start(weights(i))
    down.start()

    barrier = pltpu.get_barrier_semaphore()
    for device_id in (right, left, partner):
        pl.semaphore_signal(barrier, inc=1, device_id={AXIS: device_id}, device_id_type=MESH)
    pl.semaphore_wait(barrier, 3)

    ag_start(0, 1)
    xd(0).start()

    xd(0).wait_recv()
    load_partner = load(1, [(xg.at[partner], rows)])
    start(load_partner)
    wait(load_own)
    up(0, 0, arriving=True)

    ag_wait(0)
    ag_start(2)
    wait(load_partner)
    up(1, 1)
    down.wait()
    project(1, 0, rows, to_other(0))
    td(0, 0).start()

    ag_wait(1)
    ag_start(3, 4, 5)
    xd(1).start()
    xd(2).start()
    tile = load(0, near(k))
    start(tile)
    tile_other = load(1, near(other))

    def hook_near():
        xd(1).wait_recv()
        xd(2).wait_recv()
        start(tile_other)

    wait(tile)
    up(0, 1, hook_near)
    td(0, 0).wait_recv()
    term(0).start()
    wait(tile_other)
    up(1, 2)
    project(2, 0, rows, to_other(1))
    td(1, 1).start()
    term(0).wait()
    project(0, 0, rows, to_own)

    ag_wait(2, 3)
    xd(3).start()
    xd(4).start()
    td(1, 1).wait_recv()
    term(1).start()
    term(1).wait()
    tile_other2 = load(0, opposite(other))

    def hook_far():
        xd(3).wait_recv()
        xd(4).wait_recv()
        start(tile_other2)

    project(1, 0, rows, to_ring(2), hook_far)
    direct(0).start()
    direct(1).start()

    tile2 = load(1, opposite(k))
    start(tile2)
    wait(tile_other2)
    up(0, 0)
    td(0, 0).wait_send()
    project(0, 0, rows, to_other(0))
    td(2, 0).start()
    wait(tile2)
    up(1, 1)

    ag_wait(4, 5)
    xd(5).start()
    xd(6).start()
    td(2, 0).wait_recv()
    term(2).start()
    td(1, 1).wait_send()
    term(2).wait()
    tile_other3 = load(0, late(other))

    def hook_late():
        xd(5).wait_recv()
        xd(6).wait_recv()
        start(tile_other3)

    project(1, 0, rows, to_ring(1), hook_late)
    for j in (0, 1):
        for d in (0, 1):
            distant(d, j).start()

    tile3 = load(1, late(k))
    start(tile3)
    wait(tile_other3)
    up(0, 0)
    td(2, 0).wait_send()
    project(0, 0, rows, to_other(0))
    td(3, 0).start()
    wait(tile3)
    up(1, 1)
    td(3, 0).wait_recv()
    term(3).start()
    direct(0).wait_send()
    direct(1).wait_send()
    term(3).wait()

    for j in (0, 1):
        for d in (0, 1):
            distant(d, j).wait_recv()
        project(1, 2 * j * q, 2 * q, to_last(j))
        for d in (0, 1):
            summed(d, j).start()

    td(3, 0).wait_send()
    direct(0).wait_recv()
    direct(1).wait_recv()
    results = []
    for j in (0, 1):
        for d in (0, 1):
            summed(d, j).wait_recv()
            r = pl.ds(first(d, j), q)
            ov[0, r, :] = (own[r, :] + fv[0, r, :].astype(F32) + fv[1, r, :].astype(F32)).astype(BF16)
            copy = pltpu.make_async_copy(ov.at[0, r, :], y.at[r, :], y_sem.at[d, j])
            copy.start()
            results.append(copy)

    for t in range(6):
        for d in (0, 1):
            ag(d, t).wait_send()
    for i in range(7):
        xd(i).wait_send()
    for j in (0, 1):
        for d in (0, 1):
            distant(d, j).wait_send()
            summed(d, j).wait_send()
    wait(results)


def solution(mesh):
    n = mesh.shape[AXIS]

    def step(x, w_gate, w_up, w_down):
        rows, depth = x.shape
        ff = w_gate.shape[1]
        any_space = pl.BlockSpec(memory_space=pl.ANY)
        dma = pltpu.SemaphoreType.DMA
        out = pl.pallas_call(
            functools.partial(kernel, n),
            out_shape=(
                jax.ShapeDtypeStruct((rows, depth), BF16),
                jax.ShapeDtypeStruct((n, rows, depth), BF16),
                jax.ShapeDtypeStruct((n // 2, rows, depth), BF16),
            ),
            in_specs=[any_space] * 4,
            out_specs=(any_space,) * 3,
            scratch_shapes=[
                pltpu.VMEM((depth, ff), BF16),
                pltpu.VMEM((depth, ff), BF16),
                pltpu.VMEM((ff, depth), BF16),
                pltpu.VMEM((2, rows, depth), BF16),
                pltpu.VMEM((3, rows, ff), BF16),
                pltpu.VMEM((3, rows, depth), BF16),
                pltpu.VMEM((rows, depth), BF16),
                pltpu.VMEM((2, rows // 2, depth), BF16),
                pltpu.VMEM((2, rows, depth), BF16),
                pltpu.VMEM((rows, depth), F32),
                dma((2, ff // split(ff, 768))),
                dma,
                dma((2, 4)),
                dma,
                dma((2, 2)),
                dma((2, 6)), dma((2, 6)),
                dma((7,)), dma((7,)),
                dma((4,)), dma((4,)),
                dma((2,)), dma((2,)),
                dma((2, 2)), dma((2, 2)),
                dma((2, 2)), dma((2, 2)),
            ],
            compiler_params=pltpu.CompilerParams(
                collective_id=0, has_side_effects=True, vmem_limit_bytes=VMEM_BYTES
            ),
            name="mlp_block",
        )(x, w_gate, w_up, w_down)
        return out[0]

    return jax.shard_map(
        step,
        mesh=mesh,
        in_specs=(P(("dp", "tp"), None), P(None, "tp"), P(None, "tp"), P("tp", None)),
        out_specs=P(("dp", "tp"), None),
        check_vma=False,
    )
```

time: 290 us -> 145 us (0.50)
  waiting for transfers between devices: 175 us -> 0 us
  Pallas kernels: 0 us -> 142 us
  matrix products: 102 us -> 0 us
  between operations: 13.4 us -> 0.01 us
  local copies, waits for them, and re-layouts: 0.01 us -> 3.13 us
    pallas_call x0 -> x1, Pallas kernels: none -> 142 us  [step(): pl.pallas_call(functools.partial(kernel, n), out_shape=(jax.ShapeDtypeStr...]
    dot_general x3 -> x0, matrix products: 102 us -> none  [the longest x1 35.1 us: step(): up = jnp.dot(rows, w_up, preferred_element_type=jnp.float32)]
    reduce_scatter x1 -> x0, waiting for transfers between devices: 88.4 us -> none  [step(): return lax.psum_scatter(term, 'tp', scatter_dimension=0, tiled=True)]
    all_gather x1 -> x0, waiting for transfers between devices: 85.5 us -> none  [step(): rows = lax.all_gather(x, 'tp', axis=0, tiled=True)]
    unnamed x2 -> x1, local copies, waits for them, and re-layouts: 0.01 us -> 3.13 us
  transfers between devices with their start and end apart: 2 -> 0, of which waited for: 2 -> 0; matrix products, arithmetic and copies ran while one was open for 0% -> 0% of each run, Pallas kernels for 0% -> 0%
where the time goes in v1:
time: 145 us
  Pallas kernels  142 us (98%)
  local copies, waits for them, and re-layouts  3.13 us (2%)
    pallas_call x1, Pallas kernels, step(): pl.pallas_call(functools.partial(kernel, n), out_shape=(jax.ShapeDtypeStr...  142 us
    unnamed x1, local copies, waits for them, and re-layouts  3.13 us

profile of v1, /device:TPU:112, one launch (start us, length us, event | category | flops | bytes accessed | tf_op | source)
XLA Modules:
  0.0 145.1 jit_solution(1827673513392549029)
XLA Ops:
  0.0 142.0 %mlp_block.1 = (bf16[256,4096]{1,0:T(8,128)(2,1)}, bf16[8,256,4096]{2,1,0:T(8,128)(2,1)}, bf16[4,256,4096]{2,1,0:T(8,128)(2,1)}) custom-call(bf16[256,4096]{1,0:T(8,128)(2,1)} %x.1, bf16[4096,1536]{1,0:T(8,128)(2,1)} %wg.1, bf16[4096,1536]{1,0:T(8,128)(2,1)} %wu.1, bf16[1536,4096]{1,0:T(8,128)(2,1)} %wd.1), custom_call_target="tpu_custom_call" | custom-call | tf_op jit(solution)/shard_map/mlp_block/pallas_call | solution.py:352
  142.0 3.1 %copy.6 = bf16[256,4096]{1,0:T(8,128)(2,1)} copy(bf16[256,4096]{1,0:T(8,128)(2,1)} %get-tuple-element.6) | data formatting | bytes 4194304

commit v2 on v1

--- a/solution.py
+++ b/solution.py
@@ -11,7 +11,7 @@
 AXIS = "tp"
 F32 = jnp.float32
 BF16 = jnp.bfloat16
-VMEM_BYTES = 67043328
+VMEM_BYTES = 67043328 - 2 * 1024 * 1024
 
 
 def split(total, most):
@@ -23,7 +23,7 @@
     x, wg, wu, wd,
     y, xg, tp,
     wgv, wuv, wdv, xv, hv, ov, tv, sv, fv, own,
-    w_sem, wd_sem, x_sem, t_sem, y_sem,
+    w_sem, wd_sem, x_sem, t_sem,
     ag_send, ag_recv, xd_send, xd_recv, td_send, td_recv,
     dir_send, dir_recv, far_send, far_recv, sum_send, sum_recv,
 ):
@@ -196,15 +196,15 @@
                 ov[2, place, r] = total.astype(BF16)
         return finish
 
+    barrier = pltpu.get_barrier_semaphore()
+    for device_id in (right, left, partner):
+        pl.semaphore_signal(barrier, inc=1, device_id={AXIS: device_id}, device_id_type=MESH)
     load_own = load(0, [(x, rows)])
     start(load_own)
     for i in range(ff // nt):
         start(weights(i))
     down.start()
 
-    barrier = pltpu.get_barrier_semaphore()
-    for device_id in (right, left, partner):
-        pl.semaphore_signal(barrier, inc=1, device_id={AXIS: device_id}, device_id_type=MESH)
     pl.semaphore_wait(barrier, 3)
 
     ag_start(0, 1)
@@ -317,18 +317,6 @@
             summed(d, j).start()
 
     td(3, 0).wait_send()
-    direct(0).wait_recv()
-    direct(1).wait_recv()
-    results = []
-    for j in (0, 1):
-        for d in (0, 1):
-            summed(d, j).wait_recv()
-            r = pl.ds(first(d, j), q)
-            ov[0, r, :] = (own[r, :] + fv[0, r, :].astype(F32) + fv[1, r, :].astype(F32)).astype(BF16)
-            copy = pltpu.make_async_copy(ov.at[0, r, :], y.at[r, :], y_sem.at[d, j])
-            copy.start()
-            results.append(copy)
-
     for t in range(6):
         for d in (0, 1):
             ag(d, t).wait_send()
@@ -337,8 +325,18 @@
     for j in (0, 1):
         for d in (0, 1):
             distant(d, j).wait_send()
-            summed(d, j).wait_send()
-    wait(results)
+    direct(0).wait_recv()
+    direct(1).wait_recv()
+    for j in (0, 1):
+        for d in (0, 1):
+            if j == 1:
+                summed(d, 0).wait_send()
+            summed(d, j).wait_recv()
+            r = pl.ds(first(d, j), q)
+            y[r, :] = (own[r, :] + fv[0, r, :].astype(F32) + fv[1, r, :].astype(F32)).astype(BF16)
+
+    for d in (0, 1):
+        summed(d, 1).wait_send()
 
 
 def solution(mesh):
@@ -352,12 +350,12 @@
         out = pl.pallas_call(
             functools.partial(kernel, n),
             out_shape=(
-                jax.ShapeDtypeStruct((rows, depth), BF16),
+                pltpu.VMEM((rows, depth), BF16),
                 jax.ShapeDtypeStruct((n, rows, depth), BF16),
                 jax.ShapeDtypeStruct((n // 2, rows, depth), BF16),
             ),
             in_specs=[any_space] * 4,
-            out_specs=(any_space,) * 3,
+            out_specs=(pl.BlockSpec(memory_space=pltpu.VMEM), any_space, any_space),
             scratch_shapes=[
                 pltpu.VMEM((depth, ff), BF16),
                 pltpu.VMEM((depth, ff), BF16),
@@ -373,7 +371,6 @@
                 dma,
                 dma((2, 4)),
                 dma,
-                dma((2, 2)),
                 dma((2, 6)), dma((2, 6)),
                 dma((7,)), dma((7,)),
                 dma((4,)), dma((4,)),

time: 145 us -> 143 us (0.986)
  local copies, waits for them, and re-layouts: 3.13 us -> 1.32 us
    unnamed x1, local copies, waits for them, and re-layouts: 3.13 us -> 1.32 us
where the time goes in v2:
time: 143 us; the launch traced here: 142 us
  Pallas kernels  141 us (99%)
    pallas_call x1, Pallas kernels, step(): pl.pallas_call(functools.partial(kernel, n), out_shape=(pltpu.VMEM((rows,...  141 us

profile of v2, /device:TPU:112, one launch (start us, length us, event | category | flops | bytes accessed | tf_op | source)
XLA Modules:
  0.0 142.4 jit_solution(15088866156803230578)
XLA Ops:
  0.0 141.1 %mlp_block.1 = (bf16[256,4096]{1,0:T(8,128)(2,1)S(1)}, bf16[8,256,4096]{2,1,0:T(8,128)(2,1)}, bf16[4,256,4096]{2,1,0:T(8,128)(2,1)}) custom-call(bf16[256,4096]{1,0:T(8,128)(2,1)} %x.1, bf16[4096,1536]{1,0:T(8,128)(2,1)} %wg.1, bf16[4096,1536]{1,0:T(8,128)(2,1)} %wu.1, bf16[1536,4096]{1,0:T(8,128)(2,1)} %wd.1), custom_call_target="tpu_custom_call" | custom-call | tf_op jit(solution)/shard_map/mlp_block/pallas_call | solution.py:350
  141.1 1.3 copy.6

commit v3 on v2

--- a/solution.py
+++ b/solution.py
@@ -23,9 +23,8 @@
     x, wg, wu, wd,
     y, xg, tp,
     wgv, wuv, wdv, xv, hv, ov, tv, sv, fv, own,
-    w_sem, wd_sem, x_sem, t_sem,
-    ag_send, ag_recv, xd_send, xd_recv, td_send, td_recv,
-    dir_send, dir_recv, far_send, far_recv, sum_send, sum_recv,
+    w_sem, wd_sem, x_sem, t_sem, rows_sent, sums_sent,
+    ag_recv, xd_recv, td_send, td_recv, dir_send, dir_recv, far_recv, sum_recv,
 ):
     rows, depth = x.shape
     ff = wg.shape[1]
@@ -52,6 +51,13 @@
             device_id={AXIS: device_id}, device_id_type=MESH,
         )
 
+    def landed(sem, count):
+        if count % rows == 0:
+            ref = xg.at[pl.ds(0, count // rows)]
+        else:
+            ref = at(xg, 0, 0, count)
+        pltpu.make_async_copy(ref, ref, sem).wait()
+
     def first(d, j):
         return (0 if d == 0 else h) + j * q
 
@@ -64,15 +70,13 @@
             src = xg.at[came[d], r, :]
             dst = src
         else:
-            r = pl.ds(first(d, t) if t < 2 else second(d, t - 4), q)
+            r = pl.ds(first(d, t), q) if t < 2 else pl.ds(second(d, 0), h)
             src = x.at[r, :]
             dst = xg.at[me, r, :]
-        return remote(src, dst, ag_send.at[d, t], ag_recv.at[d, t], to[d])
-
-    def ag_wait(*ts):
-        for t in ts:
-            for d in (0, 1):
-                ag(d, t).wait_recv()
+        return remote(src, dst, rows_sent, ag_recv.at[(0, 1, 2, 2, 3)[t]], to[d])
+
+    def ag_wait(i):
+        landed(ag_recv.at[i], (2 * q, 2 * q, 4 * q, 2 * h)[i])
 
     def ag_start(*ts):
         for t in ts:
@@ -89,29 +93,32 @@
             block, start = pieces[i - 1]
             src = at(xg, block, start, h)
             dst = src
-        return remote(src, dst, xd_send.at[i], xd_recv.at[i], partner)
+        return remote(src, dst, rows_sent, xd_recv.at[(i + 1) // 2], partner)
+
+    def xd_wait(i):
+        landed(xd_recv.at[i], rows)
 
     def td(j, slot):
-        return remote(ov.at[slot], tp.at[j], td_send.at[j], td_recv.at[j], partner)
+        return remote(ov.at[slot], tp.at[j], td_send.at[slot], td_recv.at[j], partner)
 
     def direct(d):
         r = pl.ds(h, h) if d == 0 else pl.ds(0, h)
-        return remote(ov.at[2, r, :], fv.at[d, r, :], dir_send.at[d], dir_recv.at[d], to[d])
+        return remote(ov.at[2, r, :], fv.at[d, r, :], dir_send, dir_recv, to[d])
 
     def distant(d, j):
-        return remote(
-            at(ov, 1, first(d, j), q), at(sv, d, j * q, q), far_send.at[d, j], far_recv.at[d, j], to[d]
-        )
-
-    def summed(d, j):
-        return remote(
-            at(ov, 2, (2 * j + d) * q, q), at(fv, d, first(d, j), q), sum_send.at[d, j], sum_recv.at[d, j], to[d]
-        )
+        return remote(at(ov, 1, first(d, j), q), at(sv, d, j * q, q), sums_sent, far_recv.at[j], to[d])
+
+    cuts = ((0, q), (q, q // 2), (q + q // 2, q // 2))
+
+    def summed(d, i):
+        place, size = cuts[i]
+        src = at(ov, 2, (2 * (place // q) + d) * q + place % q, size)
+        return remote(src, at(fv, d, first(d, 0) + place, size), sums_sent, sum_recv.at[i], to[d])
 
     def load(slot, parts):
         out, place = [], 0
-        for i, (src, size) in enumerate(parts):
-            out.append(pltpu.make_async_copy(src, xv.at[slot, pl.ds(place, size), :], x_sem.at[slot, i]))
+        for src, size in parts:
+            out.append(pltpu.make_async_copy(src, xv.at[slot, pl.ds(place, size), :], x_sem.at[slot]))
             place += size
         return out
 
@@ -132,6 +139,9 @@
     def wait(copies):
         for copy in copies:
             copy.wait()
+
+    def loaded(slot):
+        landed(x_sem.at[slot], rows)
 
     def term(j):
         return pltpu.make_async_copy(tp.at[j], tv, t_sem)
@@ -210,22 +220,22 @@
     ag_start(0, 1)
     xd(0).start()
 
-    xd(0).wait_recv()
+    xd_wait(0)
     load_partner = load(1, [(xg.at[partner], rows)])
     start(load_partner)
-    wait(load_own)
+    loaded(0)
     up(0, 0, arriving=True)
 
     ag_wait(0)
     ag_start(2)
-    wait(load_partner)
+    loaded(1)
     up(1, 1)
     down.wait()
     project(1, 0, rows, to_other(0))
     td(0, 0).start()
 
     ag_wait(1)
-    ag_start(3, 4, 5)
+    ag_start(3, 4)
     xd(1).start()
     xd(2).start()
     tile = load(0, near(k))
@@ -233,22 +243,21 @@
     tile_other = load(1, near(other))
 
     def hook_near():
-        xd(1).wait_recv()
-        xd(2).wait_recv()
+        xd_wait(1)
         start(tile_other)
 
-    wait(tile)
+    loaded(0)
     up(0, 1, hook_near)
     td(0, 0).wait_recv()
     term(0).start()
-    wait(tile_other)
+    loaded(1)
     up(1, 2)
     project(2, 0, rows, to_other(1))
     td(1, 1).start()
     term(0).wait()
     project(0, 0, rows, to_own)
 
-    ag_wait(2, 3)
+    ag_wait(2)
     xd(3).start()
     xd(4).start()
     td(1, 1).wait_recv()
@@ -257,8 +266,7 @@
     tile_other2 = load(0, opposite(other))
 
     def hook_far():
-        xd(3).wait_recv()
-        xd(4).wait_recv()
+        xd_wait(2)
         start(tile_other2)
 
     project(1, 0, rows, to_ring(2), hook_far)
@@ -267,15 +275,15 @@
 
     tile2 = load(1, opposite(k))
     start(tile2)
-    wait(tile_other2)
+    loaded(0)
     up(0, 0)
     td(0, 0).wait_send()
     project(0, 0, rows, to_other(0))
     td(2, 0).start()
-    wait(tile2)
+    loaded(1)
     up(1, 1)
 
-    ag_wait(4, 5)
+    ag_wait(3)
     xd(5).start()
     xd(6).start()
     td(2, 0).wait_recv()
@@ -285,8 +293,7 @@
     tile_other3 = load(0, late(other))
 
     def hook_late():
-        xd(5).wait_recv()
-        xd(6).wait_recv()
+        xd_wait(3)
         start(tile_other3)
 
     project(1, 0, rows, to_ring(1), hook_late)
@@ -296,47 +303,34 @@
 
     tile3 = load(1, late(k))
     start(tile3)
-    wait(tile_other3)
+    loaded(0)
     up(0, 0)
     td(2, 0).wait_send()
     project(0, 0, rows, to_other(0))
     td(3, 0).start()
-    wait(tile3)
+    loaded(1)
     up(1, 1)
     td(3, 0).wait_recv()
     term(3).start()
-    direct(0).wait_send()
-    direct(1).wait_send()
+    landed(dir_send, rows)
     term(3).wait()
 
     for j in (0, 1):
+        landed(far_recv.at[j], 2 * q)
+        project(1, 2 * j * q, 2 * q, to_last(j))
+        for i in (0,) if j == 0 else (1, 2):
+            for d in (0, 1):
+                summed(d, i).start()
+
+    td(3, 0).wait_send()
+    landed(rows_sent, 3 * rows + 4 * rows)
+    landed(dir_recv, rows)
+    for i, (place, size) in enumerate(cuts):
+        landed(sum_recv.at[i], 2 * size)
         for d in (0, 1):
-            distant(d, j).wait_recv()
-        project(1, 2 * j * q, 2 * q, to_last(j))
-        for d in (0, 1):
-            summed(d, j).start()
-
-    td(3, 0).wait_send()
-    for t in range(6):
-        for d in (0, 1):
-            ag(d, t).wait_send()
-    for i in range(7):
-        xd(i).wait_send()
-    for j in (0, 1):
-        for d in (0, 1):
-            distant(d, j).wait_send()
-    direct(0).wait_recv()
-    direct(1).wait_recv()
-    for j in (0, 1):
-        for d in (0, 1):
-            if j == 1:
-                summed(d, 0).wait_send()
-            summed(d, j).wait_recv()
-            r = pl.ds(first(d, j), q)
+            r = pl.ds(first(d, 0) + place, size)
             y[r, :] = (own[r, :] + fv[0, r, :].astype(F32) + fv[1, r, :].astype(F32)).astype(BF16)
-
-    for d in (0, 1):
-        summed(d, 1).wait_send()
+    landed(sums_sent, 2 * rows)
 
 
 def solution(mesh):
@@ -367,16 +361,8 @@
                 pltpu.VMEM((2, rows // 2, depth), BF16),
                 pltpu.VMEM((2, rows, depth), BF16),
                 pltpu.VMEM((rows, depth), F32),
-                dma((2, ff // split(ff, 768))),
-                dma,
-                dma((2, 4)),
-                dma,
-                dma((2, 6)), dma((2, 6)),
-                dma((7,)), dma((7,)),
-                dma((4,)), dma((4,)),
-                dma((2,)), dma((2,)),
-                dma((2, 2)), dma((2, 2)),
-                dma((2, 2)), dma((2, 2)),
+                dma((2, ff // split(ff, 768))), dma, dma((2,)), dma, dma, dma,
+                dma((4,)), dma((4,)), dma((2,)), dma((4,)), dma, dma, dma((2,)), dma((3,)),
             ],
             compiler_params=pltpu.CompilerParams(
                 collective_id=0, has_side_effects=True, vmem_limit_bytes=VMEM_BYTES

time: 143 us -> 142 us (level)
  no operation moved by 1% of the time
where the time goes in v3:
time: 142 us
  Pallas kernels  140 us (99%)
    pallas_call x1, Pallas kernels, step(): pl.pallas_call(functools.partial(kernel, n), out_shape=(pltpu.VMEM((rows,...  140 us

profile of v3, /device:TPU:112, one launch (start us, length us, event | category | flops | bytes accessed | tf_op | source)
XLA Modules:
  0.0 141.8 jit_solution(6318544553170266642)
XLA Ops:
  0.0 140.5 %mlp_block.1 = (bf16[256,4096]{1,0:T(8,128)(2,1)S(1)}, bf16[8,256,4096]{2,1,0:T(8,128)(2,1)}, bf16[4,256,4096]{2,1,0:T(8,128)(2,1)}) custom-call(bf16[256,4096]{1,0:T(8,128)(2,1)} %x.1, bf16[4096,1536]{1,0:T(8,128)(2,1)} %wg.1, bf16[4096,1536]{1,0:T(8,128)(2,1)} %wu.1, bf16[1536,4096]{1,0:T(8,128)(2,1)} %wd.1), custom_call_target="tpu_custom_call" | custom-call | tf_op jit(solution)/shard_map/mlp_block/pallas_call | solution.py:344
  140.5 1.3 copy.6

commit v4 on v3

--- a/solution.py
+++ b/solution.py
@@ -21,9 +21,9 @@
 def kernel(
     n,
     x, wg, wu, wd,
-    y, xg, tp,
+    y, xg,
     wgv, wuv, wdv, xv, hv, ov, tv, sv, fv, own,
-    w_sem, wd_sem, x_sem, t_sem, rows_sent, sums_sent,
+    w_sem, wd_sem, x_sem, rows_sent, sums_sent,
     ag_recv, xd_recv, td_send, td_recv, dir_send, dir_recv, far_recv, sum_recv,
 ):
     rows, depth = x.shape
@@ -99,7 +99,7 @@
         landed(xd_recv.at[i], rows)
 
     def td(j, slot):
-        return remote(ov.at[slot], tp.at[j], td_send.at[slot], td_recv.at[j], partner)
+        return remote(ov.at[slot], tv.at[j % 2], td_send.at[slot], td_recv.at[j], partner)
 
     def direct(d):
         r = pl.ds(h, h) if d == 0 else pl.ds(0, h)
@@ -142,9 +142,6 @@
 
     def loaded(slot):
         landed(x_sem.at[slot], rows)
-
-    def term(j):
-        return pltpu.make_async_copy(tp.at[j], tv, t_sem)
 
     nt = split(ff, 768)
     dt = split(depth, 2048)
@@ -191,18 +188,18 @@
         return finish
 
     def to_own(r, acc):
-        own[:, r] = acc + tv[:, r].astype(F32)
-
-    def to_ring(slot):
+        own[:, r] = acc + tv[0, :, r].astype(F32)
+
+    def to_ring(slot, j):
         def finish(r, acc):
-            ov[slot, :, r] = (acc + tv[:, r].astype(F32)).astype(BF16)
+            ov[slot, :, r] = (acc + tv[j % 2, :, r].astype(F32)).astype(BF16)
         return finish
 
     def to_last(j):
         def finish(r, acc):
             for d in (0, 1):
                 place = pl.ds((2 * j + d) * q, q)
-                total = acc[d * q:(d + 1) * q] + tv[place, r].astype(F32) + sv[d, pl.ds(j * q, q), r].astype(F32)
+                total = acc[d * q:(d + 1) * q] + tv[1, place, r].astype(F32) + sv[d, pl.ds(j * q, q), r].astype(F32)
                 ov[2, place, r] = total.astype(BF16)
         return finish
 
@@ -249,27 +246,23 @@
     loaded(0)
     up(0, 1, hook_near)
     td(0, 0).wait_recv()
-    term(0).start()
+    project(0, 0, rows, to_own)
     loaded(1)
-    up(1, 2)
-    project(2, 0, rows, to_other(1))
+    up(1, 0)
+    project(0, 0, rows, to_other(1))
     td(1, 1).start()
-    term(0).wait()
-    project(0, 0, rows, to_own)
 
     ag_wait(2)
     xd(3).start()
     xd(4).start()
-    td(1, 1).wait_recv()
-    term(1).start()
-    term(1).wait()
     tile_other2 = load(0, opposite(other))
 
     def hook_far():
         xd_wait(2)
         start(tile_other2)
 
-    project(1, 0, rows, to_ring(2), hook_far)
+    td(1, 1).wait_recv()
+    project(1, 0, rows, to_ring(2, 1), hook_far)
     direct(0).start()
     direct(1).start()
 
@@ -287,16 +280,14 @@
     xd(5).start()
     xd(6).start()
     td(2, 0).wait_recv()
-    term(2).start()
     td(1, 1).wait_send()
-    term(2).wait()
     tile_other3 = load(0, late(other))
 
     def hook_late():
         xd_wait(3)
         start(tile_other3)
 
-    project(1, 0, rows, to_ring(1), hook_late)
+    project(1, 0, rows, to_ring(1, 2), hook_late)
     for j in (0, 1):
         for d in (0, 1):
             distant(d, j).start()
@@ -311,9 +302,7 @@
     loaded(1)
     up(1, 1)
     td(3, 0).wait_recv()
-    term(3).start()
     landed(dir_send, rows)
-    term(3).wait()
 
     for j in (0, 1):
         landed(far_recv.at[j], 2 * q)
@@ -346,22 +335,21 @@
             out_shape=(
                 pltpu.VMEM((rows, depth), BF16),
                 jax.ShapeDtypeStruct((n, rows, depth), BF16),
-                jax.ShapeDtypeStruct((n // 2, rows, depth), BF16),
             ),
             in_specs=[any_space] * 4,
-            out_specs=(pl.BlockSpec(memory_space=pltpu.VMEM), any_space, any_space),
+            out_specs=(pl.BlockSpec(memory_space=pltpu.VMEM), any_space),
             scratch_shapes=[
                 pltpu.VMEM((depth, ff), BF16),
                 pltpu.VMEM((depth, ff), BF16),
                 pltpu.VMEM((ff, depth), BF16),
                 pltpu.VMEM((2, rows, depth), BF16),
-                pltpu.VMEM((3, rows, ff), BF16),
+                pltpu.VMEM((2, rows, ff), BF16),
                 pltpu.VMEM((3, rows, depth), BF16),
-                pltpu.VMEM((rows, depth), BF16),
+                pltpu.VMEM((2, rows, depth), BF16),
                 pltpu.VMEM((2, rows // 2, depth), BF16),
                 pltpu.VMEM((2, rows, depth), BF16),
                 pltpu.VMEM((rows, depth), F32),
-                dma((2, ff // split(ff, 768))), dma, dma((2,)), dma, dma, dma,
+                dma((2, ff // split(ff, 768))), dma, dma((2,)), dma, dma,
                 dma((4,)), dma((4,)), dma((2,)), dma((4,)), dma, dma, dma((2,)), dma((3,)),
             ],
             compiler_params=pltpu.CompilerParams(

time: 142 us -> 142 us (level)
  no operation moved by 1% of the time
where the time goes in v4:
time: 142 us
  Pallas kernels  140 us (99%)
    pallas_call x1, Pallas kernels, step(): pl.pallas_call(functools.partial(kernel, n), out_shape=(pltpu.VMEM((rows,...  140 us

profile of v4, /device:TPU:112, one launch (start us, length us, event | category | flops | bytes accessed | tf_op | source)
XLA Modules:
  0.0 141.8 jit_solution(15382053424216609838)
XLA Ops:
  0.0 140.5 %mlp_block.1 = (bf16[256,4096]{1,0:T(8,128)(2,1)S(1)}, bf16[8,256,4096]{2,1,0:T(8,128)(2,1)}) custom-call(bf16[256,4096]{1,0:T(8,128)(2,1)} %x.1, bf16[4096,1536]{1,0:T(8,128)(2,1)} %wg.1, bf16[4096,1536]{1,0:T(8,128)(2,1)} %wu.1, bf16[1536,4096]{1,0:T(8,128)(2,1)} %wd.1), custom_call_target="tpu_custom_call" | custom-call | tf_op jit(solution)/shard_map/mlp_block/pallas_call | solution.py:333
  140.5 1.3 copy.6

commit v5 on v4

--- a/solution.py
+++ b/solution.py
@@ -99,7 +99,7 @@
         landed(xd_recv.at[i], rows)
 
     def td(j, slot):
-        return remote(ov.at[slot], tv.at[j % 2], td_send.at[slot], td_recv.at[j], partner)
+        return remote(ov.at[slot], tv.at[j % 2], td_send, td_recv.at[j % 2], partner)
 
     def direct(d):
         r = pl.ds(h, h) if d == 0 else pl.ds(0, h)
@@ -108,7 +108,7 @@
     def distant(d, j):
         return remote(at(ov, 1, first(d, j), q), at(sv, d, j * q, q), sums_sent, far_recv.at[j], to[d])
 
-    cuts = ((0, q), (q, q // 2), (q + q // 2, q // 2))
+    cuts = ((0, q), (q, 3 * q // 4), (q + 3 * q // 4, q // 4))
 
     def summed(d, i):
         place, size = cuts[i]
@@ -149,8 +149,8 @@
     def weights(i):
         r = pl.ds(pl.multiple_of(i * nt, nt), nt)
         return [
-            pltpu.make_async_copy(wg.at[:, r], wgv.at[:, r], w_sem.at[0, i]),
-            pltpu.make_async_copy(wu.at[:, r], wuv.at[:, r], w_sem.at[1, i]),
+            pltpu.make_async_copy(wg.at[:, r], wgv.at[:, r], w_sem.at[i]),
+            pltpu.make_async_copy(wu.at[:, r], wuv.at[:, r], w_sem.at[i]),
         ]
 
     down = pltpu.make_async_copy(wd, wdv, wd_sem)
@@ -158,7 +158,8 @@
     def up(slot, hslot, hook=None, arriving=False):
         def body(i, carry):
             if arriving:
-                wait(weights(i))
+                both = wgv.at[:, pl.ds(0, 2 * nt)]
+                pltpu.make_async_copy(both, both, w_sem.at[i]).wait()
             if hook is not None:
                 pl.when(i == ff // nt - 1)(hook)
             for s in range(0, nt, 256):
@@ -250,6 +251,7 @@
     loaded(1)
     up(1, 0)
     project(0, 0, rows, to_other(1))
+    td(0, 0).wait_send()
     td(1, 1).start()
 
     ag_wait(2)
@@ -270,8 +272,8 @@
     start(tile2)
     loaded(0)
     up(0, 0)
-    td(0, 0).wait_send()
     project(0, 0, rows, to_other(0))
+    td(1, 1).wait_send()
     td(2, 0).start()
     loaded(1)
     up(1, 1)
@@ -280,7 +282,6 @@
     xd(5).start()
     xd(6).start()
     td(2, 0).wait_recv()
-    td(1, 1).wait_send()
     tile_other3 = load(0, late(other))
 
     def hook_late():
@@ -349,8 +350,8 @@
                 pltpu.VMEM((2, rows // 2, depth), BF16),
                 pltpu.VMEM((2, rows, depth), BF16),
                 pltpu.VMEM((rows, depth), F32),
-                dma((2, ff // split(ff, 768))), dma, dma((2,)), dma, dma,
-                dma((4,)), dma((4,)), dma((2,)), dma((4,)), dma, dma, dma((2,)), dma((3,)),
+                dma((ff // split(ff, 768),)), dma, dma((2,)), dma, dma,
+                dma((4,)), dma((4,)), dma, dma((2,)), dma, dma, dma((2,)), dma((3,)),
             ],
             compiler_params=pltpu.CompilerParams(
                 collective_id=0, has_side_effects=True, vmem_limit_bytes=VMEM_BYTES

time: 142 us -> 142 us (level)
  no operation moved by 1% of the time
where the time goes in v5:
time: 142 us
  Pallas kernels  140 us (99%)
    pallas_call x1, Pallas kernels, step(): pl.pallas_call(functools.partial(kernel, n), out_shape=(pltpu.VMEM((rows,...  140 us

profile of v5, /device:TPU:112, one launch (start us, length us, event | category | flops | bytes accessed | tf_op | source)
XLA Modules:
  0.0 141.7 jit_solution(11618825626093290419)
XLA Ops:
  0.0 140.4 %mlp_block.1 = (bf16[256,4096]{1,0:T(8,128)(2,1)S(1)}, bf16[8,256,4096]{2,1,0:T(8,128)(2,1)}) custom-call(bf16[256,4096]{1,0:T(8,128)(2,1)} %x.1, bf16[4096,1536]{1,0:T(8,128)(2,1)} %wg.1, bf16[4096,1536]{1,0:T(8,128)(2,1)} %wu.1, bf16[1536,4096]{1,0:T(8,128)(2,1)} %wd.1), custom_call_target="tpu_custom_call" | custom-call | tf_op jit(solution)/shard_map/mlp_block/pallas_call | solution.py:334
  140.4 1.3 copy.6

commit v6 on v5

--- a/solution.py
+++ b/solution.py
@@ -23,8 +23,7 @@
     x, wg, wu, wd,
     y, xg,
     wgv, wuv, wdv, xv, hv, ov, tv, sv, fv, own,
-    w_sem, wd_sem, x_sem, rows_sent, sums_sent,
-    ag_recv, xd_recv, td_send, td_recv, dir_send, dir_recv, far_recv, sum_recv,
+    w_sem, x_sem, rows_sent, sums_sent, ag_recv, xd_recv, td_send, td_recv, dir_recv,
 ):
     rows, depth = x.shape
     ff = wg.shape[1]
@@ -93,32 +92,33 @@
             block, start = pieces[i - 1]
             src = at(xg, block, start, h)
             dst = src
-        return remote(src, dst, rows_sent, xd_recv.at[(i + 1) // 2], partner)
+        return remote(src, dst, rows_sent, xd_recv.at[(i + 1) // 2 % 2], partner)
 
     def xd_wait(i):
-        landed(xd_recv.at[i], rows)
+        landed(xd_recv.at[i % 2], rows)
 
     def td(j, slot):
         return remote(ov.at[slot], tv.at[j % 2], td_send, td_recv.at[j % 2], partner)
 
     def direct(d):
         r = pl.ds(h, h) if d == 0 else pl.ds(0, h)
-        return remote(ov.at[2, r, :], fv.at[d, r, :], dir_send, dir_recv, to[d])
+        return remote(ov.at[2, r, :], fv.at[d, r, :], rows_sent, dir_recv, to[d])
 
     def distant(d, j):
-        return remote(at(ov, 1, first(d, j), q), at(sv, d, j * q, q), sums_sent, far_recv.at[j], to[d])
-
+        return remote(at(ov, 1, first(d, j), q), at(sv, d, j * q, q), sums_sent, ag_recv.at[j], to[d])
+
+    sum_recv = (ag_recv.at[2], ag_recv.at[3], xd_recv.at[0])
     cuts = ((0, q), (q, 3 * q // 4), (q + 3 * q // 4, q // 4))
 
     def summed(d, i):
         place, size = cuts[i]
         src = at(ov, 2, (2 * (place // q) + d) * q + place % q, size)
-        return remote(src, at(fv, d, first(d, 0) + place, size), sums_sent, sum_recv.at[i], to[d])
+        return remote(src, at(fv, d, first(d, 0) + place, size), sums_sent, sum_recv[i], to[d])
 
     def load(slot, parts):
         out, place = [], 0
         for src, size in parts:
-            out.append(pltpu.make_async_copy(src, xv.at[slot, pl.ds(place, size), :], x_sem.at[slot]))
+            out.append(pltpu.make_async_copy(src, xv.at[slot, pl.ds(place, size), :], x_sem))
             place += size
         return out
 
@@ -140,8 +140,8 @@
         for copy in copies:
             copy.wait()
 
-    def loaded(slot):
-        landed(x_sem.at[slot], rows)
+    def loaded():
+        landed(x_sem, rows)
 
     nt = split(ff, 768)
     dt = split(depth, 2048)
@@ -153,13 +153,14 @@
             pltpu.make_async_copy(wu.at[:, r], wuv.at[:, r], w_sem.at[i]),
         ]
 
-    down = pltpu.make_async_copy(wd, wdv, wd_sem)
+    down = pltpu.make_async_copy(wd, wdv, w_sem.at[0])
 
     def up(slot, hslot, hook=None, arriving=False):
         def body(i, carry):
             if arriving:
                 both = wgv.at[:, pl.ds(0, 2 * nt)]
                 pltpu.make_async_copy(both, both, w_sem.at[i]).wait()
+                pl.when(i == 0)(down.start)
             if hook is not None:
                 pl.when(i == ff // nt - 1)(hook)
             for s in range(0, nt, 256):
@@ -211,7 +212,6 @@
     start(load_own)
     for i in range(ff // nt):
         start(weights(i))
-    down.start()
 
     pl.semaphore_wait(barrier, 3)
 
@@ -220,13 +220,13 @@
 
     xd_wait(0)
     load_partner = load(1, [(xg.at[partner], rows)])
+    loaded()
     start(load_partner)
-    loaded(0)
     up(0, 0, arriving=True)
 
     ag_wait(0)
     ag_start(2)
-    loaded(1)
+    loaded()
     up(1, 1)
     down.wait()
     project(1, 0, rows, to_other(0))
@@ -244,11 +244,11 @@
         xd_wait(1)
         start(tile_other)
 
-    loaded(0)
+    loaded()
     up(0, 1, hook_near)
     td(0, 0).wait_recv()
     project(0, 0, rows, to_own)
-    loaded(1)
+    loaded()
     up(1, 0)
     project(0, 0, rows, to_other(1))
     td(0, 0).wait_send()
@@ -269,13 +269,13 @@
     direct(1).start()
 
     tile2 = load(1, opposite(k))
+    loaded()
     start(tile2)
-    loaded(0)
     up(0, 0)
     project(0, 0, rows, to_other(0))
     td(1, 1).wait_send()
     td(2, 0).start()
-    loaded(1)
+    loaded()
     up(1, 1)
 
     ag_wait(3)
@@ -294,29 +294,28 @@
             distant(d, j).start()
 
     tile3 = load(1, late(k))
+    loaded()
     start(tile3)
-    loaded(0)
     up(0, 0)
     td(2, 0).wait_send()
     project(0, 0, rows, to_other(0))
     td(3, 0).start()
-    loaded(1)
+    loaded()
     up(1, 1)
     td(3, 0).wait_recv()
-    landed(dir_send, rows)
+    landed(rows_sent, (3 + 4 + 1) * rows)
 
     for j in (0, 1):
-        landed(far_recv.at[j], 2 * q)
+        landed(ag_recv.at[j], 2 * q)
         project(1, 2 * j * q, 2 * q, to_last(j))
         for i in (0,) if j == 0 else (1, 2):
             for d in (0, 1):
                 summed(d, i).start()
 
     td(3, 0).wait_send()
-    landed(rows_sent, 3 * rows + 4 * rows)
     landed(dir_recv, rows)
     for i, (place, size) in enumerate(cuts):
-        landed(sum_recv.at[i], 2 * size)
+        landed(sum_recv[i], 2 * size)
         for d in (0, 1):
             r = pl.ds(first(d, 0) + place, size)
             y[r, :] = (own[r, :] + fv[0, r, :].astype(F32) + fv[1, r, :].astype(F32)).astype(BF16)
@@ -350,8 +349,7 @@
                 pltpu.VMEM((2, rows // 2, depth), BF16),
                 pltpu.VMEM((2, rows, depth), BF16),
                 pltpu.VMEM((rows, depth), F32),
-                dma((ff // split(ff, 768),)), dma, dma((2,)), dma, dma,
-                dma((4,)), dma((4,)), dma, dma((2,)), dma, dma, dma((2,)), dma((3,)),
+                dma((ff // split(ff, 768),)), dma, dma, dma, dma((4,)), dma((2,)), dma, dma((2,)), dma,
             ],
             compiler_params=pltpu.CompilerParams(
                 collective_id=0, has_side_effects=True, vmem_limit_bytes=VMEM_BYTES

time: 142 us -> 142 us (level)
  no operation moved by 1% of the time
where the time goes in v6:
time: 142 us
  Pallas kernels  140 us (99%)
    pallas_call x1, Pallas kernels, step(): pl.pallas_call(functools.partial(kernel, n), out_shape=(pltpu.VMEM((rows,...  140 us

profile of v6, /device:TPU:112, one launch (start us, length us, event | category | flops | bytes accessed | tf_op | source)
XLA Modules:
  0.0 141.6 jit_solution(1520810383610927270)
XLA Ops:
  0.0 140.3 %mlp_block.1 = (bf16[256,4096]{1,0:T(8,128)(2,1)S(1)}, bf16[8,256,4096]{2,1,0:T(8,128)(2,1)}) custom-call(bf16[256,4096]{1,0:T(8,128)(2,1)} %x.1, bf16[4096,1536]{1,0:T(8,128)(2,1)} %wg.1, bf16[4096,1536]{1,0:T(8,128)(2,1)} %wu.1, bf16[1536,4096]{1,0:T(8,128)(2,1)} %wd.1), custom_call_target="tpu_custom_call" | custom-call | tf_op jit(solution)/shard_map/mlp_block/pallas_call | solution.py:333
  140.3 1.3 copy.6

commit v7 on v6

--- a/solution.py
+++ b/solution.py
@@ -98,7 +98,7 @@
         landed(xd_recv.at[i % 2], rows)
 
     def td(j, slot):
-        return remote(ov.at[slot], tv.at[j % 2], td_send, td_recv.at[j % 2], partner)
+        return remote(ov.at[slot], tv.at[j % 2], td_send, w_sem.at[1] if j % 2 else td_recv, partner)
 
     def direct(d):
         r = pl.ds(h, h) if d == 0 else pl.ds(0, h)
@@ -124,6 +124,11 @@
 
     def near(core):
         return [(at(xg, device(-1, core), 0, h), h), (at(xg, device(1, core), h, h), h)]
+
+    def near_part(j):
+        return [
+            pltpu.make_async_copy(at(xg, came[d], first(d, j), q), at(xv, 0, first(d, j), q), x_sem) for d in (0, 1)
+        ]
 
     def opposite(core):
         return [(xg.at[device(2, core)], rows)]
@@ -227,6 +232,7 @@
     ag_wait(0)
     ag_start(2)
     loaded()
+    start(near_part(0))
     up(1, 1)
     down.wait()
     project(1, 0, rows, to_other(0))
@@ -236,8 +242,7 @@
     ag_start(3, 4)
     xd(1).start()
     xd(2).start()
-    tile = load(0, near(k))
-    start(tile)
+    start(near_part(1))
     tile_other = load(1, near(other))
 
     def hook_near():
@@ -349,7 +354,7 @@
                 pltpu.VMEM((2, rows // 2, depth), BF16),
                 pltpu.VMEM((2, rows, depth), BF16),
                 pltpu.VMEM((rows, depth), F32),
-                dma((ff // split(ff, 768),)), dma, dma, dma, dma((4,)), dma((2,)), dma, dma((2,)), dma,
+                dma((ff // split(ff, 768),)), dma, dma, dma, dma((4,)), dma((2,)), dma, dma, dma,
             ],
             compiler_params=pltpu.CompilerParams(
                 collective_id=0, has_side_effects=True, vmem_limit_bytes=VMEM_BYTES

time: 142 us -> 142 us (level)
  no operation moved by 1% of the time
where the time goes in v7:
time: 142 us
  Pallas kernels  140 us (99%)
    pallas_call x1, Pallas kernels, step(): pl.pallas_call(functools.partial(kernel, n), out_shape=(pltpu.VMEM((rows,...  140 us

profile of v7, /device:TPU:112, one launch (start us, length us, event | category | flops | bytes accessed | tf_op | source)
XLA Modules:
  0.0 141.6 jit_solution(14235994689711714652)
XLA Ops:
  0.0 140.3 %mlp_block.1 = (bf16[256,4096]{1,0:T(8,128)(2,1)S(1)}, bf16[8,256,4096]{2,1,0:T(8,128)(2,1)}) custom-call(bf16[256,4096]{1,0:T(8,128)(2,1)} %x.1, bf16[4096,1536]{1,0:T(8,128)(2,1)} %wg.1, bf16[4096,1536]{1,0:T(8,128)(2,1)} %wu.1, bf16[1536,4096]{1,0:T(8,128)(2,1)} %wd.1), custom_call_target="tpu_custom_call" | custom-call | tf_op jit(solution)/shard_map/mlp_block/pallas_call | solution.py:338
  140.3 1.3 copy.6
